TPU v7x, 32 devices: a whole 2x2x4 slice. The times are simulated.
32 devices in a mesh: dom: 8 (over y, x, core), tp: 4 (over z).
Axes of the slice: x: 2, y: 2, z: 4, core: 2. Of those that a mesh axis runs over, the one named last changes fastest.
Arguments:
- activations: bfloat16 [4, 128, 4096], P(None, 'dom', 'tp'), may hold values from -6 to 6
- norm_gain: float32 [4096], replicated, may hold values from 0.5 to 1.5
- w_query: bfloat16 [4096, 4096], P(None, 'tp'), may hold values from -0.09375 to 0.09375
- w_key: bfloat16 [4096, 1024], P(None, 'tp'), may hold values from -0.09375 to 0.09375
- value_weight: bfloat16 [4096, 1024], P(None, 'tp'), may hold values from -0.5 to 0.5
- w_output: bfloat16 [4096, 4096], P('tp'), may hold values from -0.09375 to 0.09375
- cache_keys: bfloat16 [128, 128, 1024], P('dom', None, 'tp'), may hold values from -740 to 740
- cache_values: bfloat16 [128, 128, 1024], P('dom', None, 'tp'), may hold values from -48 to 48
- tokens: int32 [4, 128], P(None, 'dom'), may hold values from 0 to 128255
- twisting_table: bfloat16 [128256], replicated, may hold values from -6 to 6
- twist_vec: float32 [4096], P('tp'), may hold values from -0.09375 to 0.09375
- previous_log_weights: float32 [128], P('dom'), may hold values from -300 to 0
- copy_counts: int32 [128], P('dom'), may hold values from 0 to 4, as said below
Outputs:
- attn_out: bfloat16 [4, 128, 4096], P(None, 'dom', 'tp')
- new_keys: bfloat16 [128, 132, 1024], P('dom', None, 'tp')
- new_values: bfloat16 [128, 132, 1024], P('dom', None, 'tp')
- out_logw: float32 [128], P('dom')
Inputs may be any that keep to these rules, and one draw needn't show every extreme that they name: copy_counts sum to 128; the particles of one index of dom have together at most 64 copies, and one index has exactly that many.
All inputs are finite; a program needn't handle non-finite values.
Results may differ from a plain program's by a relative error of at most 0.012.
The roundings to bfloat16 on the way count: a program that leaves them out, or rounds other values in their place, can miss the bound.
Values may be sent and summed in bfloat16 or wider, within the bound.
A program may use at most 128 MiB of HBM per device.

v0:
```python
import jax
import jax.numpy as jnp
from jax import lax
from jax.sharding import PartitionSpec as P

D = 4096
HD = 128


def entering(part, axis, combine, identity):
    place = lax.axis_index(axis)
    gathered = lax.all_gather(part, axis)
    state = jnp.zeros_like(part) + jnp.asarray(identity, part.dtype)

    def one(lap, state):
        return combine(state, lax.dynamic_index_in_dim(gathered, lap, 0, False))

    return lax.fori_loop(0, place, one, state)


def rotate(tensor, positions):
    middle = tensor.shape[-1] // 2
    frequency = 500000.0 ** (-2.0 * jnp.arange(middle, dtype=jnp.float32) / tensor.shape[-1])
    angles = positions[:, None] * frequency[None, :]
    cosine = jnp.cos(angles)[:, None, None, :]
    sine_part = jnp.sin(angles)[:, None, None, :]
    lower_half = tensor[..., :middle]
    upper_half = tensor[..., middle:]
    return jnp.concatenate(
        [
            lower_half * cosine - upper_half * sine_part,
            upper_half * cosine + lower_half * sine_part,
        ],
        -1,
    )


def add_counts(former, latter):
    return former + latter


def local(
    activations,
    norm_gain,
    w_query,
    w_key,
    value_weight,
    w_output,
    cache_keys,
    cache_values,
    tokens,
    twisting_table,
    twist_vec,
    previous_log_weights,
    copy_counts,
):
    step_count = activations.shape[0]
    particle_count = activations.shape[1]
    span_old = cache_keys.shape[1]
    dom_size = lax.axis_size("dom")
    kv_local = w_key.shape[1] // HD
    q_local = w_query.shape[1] // HD
    group_size = q_local // kv_local
    capacity = 4 * particle_count // dom_size
    total_copies = jnp.sum(copy_counts)
    offset = entering(total_copies, "dom", add_counts, jnp.int32(0))
    starts = jnp.cumsum(copy_counts) - copy_counts
    position = jnp.arange(dom_size * capacity, dtype=jnp.int32)
    target = position // capacity
    copy_rank = position % capacity * dom_size + (target - offset) % dom_size
    is_live = copy_rank < total_copies
    source = jnp.sum((starts[None, :] <= copy_rank[:, None]).astype(jnp.int32), 1) - 1
    arrival = jnp.where(is_live, (offset + copy_rank) // dom_size, particle_count).astype(
        jnp.bfloat16
    )

    def pack_rows(tensor):
        return jnp.where(is_live[:, None, None], tensor[source], jnp.zeros((), tensor.dtype))

    def place_rows(tensor, slot_index):
        blank = jnp.zeros((particle_count,) + tensor.shape[1:], tensor.dtype)
        return blank.at[slot_index].set(tensor, mode="drop")

    gathered = lax.all_gather(activations, "tp", axis=2, tiled=True)
    inputs = gathered.astype(jnp.float32)
    normed = (
        inputs * lax.rsqrt(jnp.mean(inputs * inputs, -1, keepdims=True) + 1e-05) * norm_gain
    ).astype(jnp.bfloat16)
    flat_rows = normed.reshape(step_count * particle_count, D)
    positions = (span_old + jnp.arange(step_count, dtype=jnp.int32)).astype(jnp.float32)
    queries = jnp.dot(flat_rows, w_query, preferred_element_type=jnp.float32).reshape(
        step_count, particle_count, q_local, HD
    )
    queries = rotate(queries, positions).astype(jnp.bfloat16)
    fresh_keys = jnp.dot(flat_rows, w_key, preferred_element_type=jnp.float32).reshape(
        step_count, particle_count, kv_local, HD
    )
    fresh_keys = (
        rotate(fresh_keys, positions)
        .astype(jnp.bfloat16)
        .reshape(step_count, particle_count, kv_local * HD)
    )
    fresh_values = jnp.dot(flat_rows, value_weight, preferred_element_type=jnp.float32).astype(
        jnp.bfloat16
    )
    fresh_values = fresh_values.reshape(step_count, particle_count, kv_local * HD)
    fresh_keys = jnp.transpose(fresh_keys, (1, 0, 2))
    fresh_values = jnp.transpose(fresh_values, (1, 0, 2))
    key_rows = jnp.concatenate([cache_keys, fresh_keys], 1)
    value_rows = jnp.concatenate([cache_values, fresh_values], 1)
    key_span = span_old + step_count
    query_heads = queries.reshape(step_count, particle_count, kv_local, group_size, HD)
    key_heads = key_rows.reshape(particle_count, key_span, kv_local, HD)
    value_heads = value_rows.reshape(particle_count, key_span, kv_local, HD)
    scores = (
        jnp.einsum("snkgd,nlkd->snkgl", query_heads, key_heads, preferred_element_type=jnp.float32)
        / HD**0.5
    )
    allowed = (
        jnp.arange(key_span, dtype=jnp.int32)[None, :]
        <= (span_old + jnp.arange(step_count, dtype=jnp.int32))[:, None]
    )
    allowed = allowed[:, None, None, None, :]
    masked = jnp.where(allowed, scores, -jnp.inf)
    highest = jnp.max(masked, -1, keepdims=True)
    exponent = jnp.exp(masked - highest)
    weights = (exponent / jnp.sum(exponent, -1, keepdims=True)).astype(jnp.bfloat16)
    context = jnp.einsum(
        "snkgl,nlkd->snkgd", weights, value_heads, preferred_element_type=jnp.float32
    ).astype(jnp.bfloat16)
    context = context.reshape(step_count * particle_count, q_local * HD)
    partial_value = jnp.dot(context, w_output, preferred_element_type=jnp.float32).reshape(
        step_count, particle_count, D
    )
    head_mix = lax.psum_scatter(partial_value, "tp", scatter_dimension=2, tiled=True)
    attn_out = head_mix.astype(jnp.bfloat16)
    summed = activations.astype(jnp.float32) + head_mix
    aligned, energy = lax.psum(
        (jnp.sum(summed * twist_vec, -1), jnp.sum(summed * summed, -1)), "tp"
    )
    twisting_score = aligned / jnp.sqrt(energy / D + 1e-06)
    token_reward = twisting_table[tokens].astype(jnp.float32)
    particle_log_weight = previous_log_weights + jnp.sum(token_reward + twisting_score, 0)
    largest = lax.pmax(jnp.max(particle_log_weight), "dom")
    mass_total = lax.psum(jnp.sum(jnp.exp(particle_log_weight - largest)), "dom")
    out_logw = particle_log_weight - (largest + jnp.log(mass_total))
    moved_keys, moved_values, arrived = (
        lax.all_to_all(pack_rows(key_rows), "dom", split_axis=0, concat_axis=0, tiled=True),
        lax.all_to_all(pack_rows(value_rows), "dom", split_axis=0, concat_axis=0, tiled=True),
        lax.all_to_all(arrival, "dom", split_axis=0, concat_axis=0, tiled=True),
    )
    slot_index = arrived.astype(jnp.int32)
    new_keys = place_rows(moved_keys, slot_index)
    new_values = place_rows(moved_values, slot_index)
    return (attn_out, new_keys, new_values, out_logw)


def solution(mesh):
    return jax.shard_map(
        local,
        mesh=mesh,
        in_specs=(
            P(None, "dom", "tp"),
            P(),
            P(None, "tp"),
            P(None, "tp"),
            P(None, "tp"),
            P("tp", None),
            P("dom", None, "tp"),
            P("dom", None, "tp"),
            P(None, "dom"),
            P(),
            P("tp"),
            P("dom"),
            P("dom"),
        ),
        out_specs=(P(None, "dom", "tp"), P("dom", None, "tp"), P("dom", None, "tp"), P("dom")),
        check_vma=False,
    )
```

profile of v0, /device:TPU:0, one launch (start us, length us, event | category | flops | bytes accessed | tf_op | source)
XLA Modules:
  0.0 234.3 jit_solution(9963035594114682076)
XLA Ops:
  7.2 0.9 copy.65
  8.2 1.3 fusion.34
  9.5 1.2 dynamic-slice
  10.8 1.4 dynamic-update-slice
  12.2 9.5 %all-reduce = s32[8]{0:T(128)S(1)} all-reduce(s32[8]{0:T(128)S(1)} %dynamic-update-slice), channel_id=1, replica_groups=mesh['dom'=8,'tp'=4] {'dom'}, use_global_device_ids=true, to_apply=%add | all-reduce | flops 8 | bytes 64
  21.7 1.3 fusion.23
  22.9 10.4 %all-to-all-start = ((bf16[8,8,1]{1,2,0:T(2,128)(2,1)}), bf16[8,8,1]{1,2,0:T(2,128)(2,1)S(1)}, u32[]{:S(2)}, u32[]{:S(2)}) async-start(bf16[8,8,1]{1,2,0:T(2,128)(2,1)} %fusion.23), calls=%async_computation.1 | async-start | bytes 8192 | tf_op jit(solution)/shard_map/all_to_all | solution.py:150
  34.0 16.7 %all_gather.9 = bf16[4,16,4096]{2,1,0:T(8,128)(2,1)S(1)} all-gather(bf16[4,16,1024]{2,1,0:T(8,128)(2,1)} %param.15), channel_id=1, replica_groups=mesh['dom'=8,'tp'=4] {'tp'}, dimensions={2}, use_global_device_ids=true | all-gather | bytes 655360 | tf_op jit(solution)/shard_map/all_gather | solution.py:84
  50.9 4.1 %copy.75 = bf16[256,4096]{1,0:T(8,128)(2,1)} copy(bf16[256,4096]{0,1:T(8,128)(2,1)} %bitcast.59) | data formatting | bytes 4194304 | tf_op jit(solution)/shard_map/dot_general | solution.py:95
  55.3 2.5 %fusion.15 = f32[4,16,2,128]{3,1,2,0:T(8,128)S(1)} fusion(bf16[2,128,4096,1]{2,1,0,3:T(8,128)(2,1)} %bitcast.60, bf16[4,16,4096]{2,1,0:T(8,128)(2,1)S(1)} %fusion.12), kind=kOutput, calls=%fused_computation.29 | convolution fusion | flops 134217728 | bytes 2686976 | tf_op jit(solution)/shard_map/dot_general | solution.py:95
  59.8 2.9 %gather_fusion = bf16[64,132,256]{2,1,0:T(8,128)(2,1)} fusion(bf16[16,132,256]{2,1,0:T(8,128)(2,1)S(1)} %pad_maximum_fusion.1, s32[1024]{0:T(1024)S(1)} %pad_clamp_fusion.1), kind=kCustom, calls=%fused_computation | custom fusion | bytes 8651008 | tf_op jit(solution)/shard_map/gather | solution.py:78
  62.7 2.9 %gather_fusion.1 = bf16[64,132,256]{2,1,0:T(8,128)(2,1)} fusion(bf16[16,132,256]{2,1,0:T(8,128)(2,1)S(1)} %pad_maximum_fusion, s32[1024]{0:T(1024)S(1)} %pad_clamp_fusion.1), kind=kCustom, calls=%fused_computation.1 | custom fusion | bytes 8651008 | tf_op jit(solution)/shard_map/gather | solution.py:78
  65.6 7.6 %broadcast_select_fusion = (bf16[64,132,256]{2,1,0:T(8,128)(2,1)}, bf16[64,132,256]{2,1,0:T(8,128)(2,1)}) fusion(bf16[64,132,256]{2,1,0:T(8,128)(2,1)} %gather_fusion.1, pred[64]{0:T(512)(128)(4,1)S(1)} %broadcast_compare_fusion, bf16[64,132,256]{2,1,0:T(8,128)(2,1)} %gather_fusion), kind=kLoop, calls=%fused_computation.8 | loop fusion | flops 4325376 | bytes 17301568 | tf_op jit(solution)/shard_map/jit(_where)/select_n | solution.py:78
  73.2 4.6 %all-to-all-start.1 = ((bf16[64,132,256]{2,1,0:T(8,128)(2,1)}), bf16[64,132,256]{2,1,0:T(8,128)(2,1)}, u32[]{:S(2)}, u32[]{:S(2)}) async-start(bf16[64,132,256]{2,1,0:T(8,128)(2,1)} %get-tuple-element.62), calls=%async_computation.2 | async-start | bytes 8912896 | tf_op jit(solution)/shard_map/all_to_all | solution.py:148
  77.9 1.2 reshape.513
  79.4 11.3 %copy.81 = bf16[1024,4096]{1,0:T(8,128)(2,1)} copy(bf16[1024,4096]{0,1:T(8,128)(2,1)} %bitcast.57) | data formatting | bytes 16777216 | tf_op jit(solution)/shard_map/dot_general | solution.py:91
  90.7 6.1 %fusion.13 = f32[4,16,8,128]{3,1,2,0:T(8,128)S(1)} fusion(bf16[8,128,4096,1]{2,1,0,3:T(8,128)(2,1)} %bitcast.58, bf16[4,16,4096]{2,1,0:T(8,128)(2,1)S(1)} %copy-done.4), kind=kOutput, calls=%fused_computation.27 | convolution fusion | flops 536870912 | bytes 9175040 | tf_op jit(solution)/shard_map/dot_general | solution.py:91
  97.2 1.8 fusion.35
  99.0 30.7 %all-to-all-done.1 = bf16[64,132,256]{2,1,0:T(8,128)(2,1)} async-done(((bf16[64,132,256]{2,1,0:T(8,128)(2,1)}), bf16[64,132,256]{2,1,0:T(8,128)(2,1)}, u32[]{:S(2)}, u32[]{:S(2)}) %all-to-all-start.1) | async-done | bytes 4325408 | tf_op jit(solution)/shard_map/all_to_all | solution.py:148
  129.8 4.7 %all-to-all-start.2 = ((bf16[64,132,256]{2,1,0:T(8,128)(2,1)}), bf16[64,132,256]{2,1,0:T(8,128)(2,1)}, u32[]{:S(2)}, u32[]{:S(2)}) async-start(bf16[64,132,256]{2,1,0:T(8,128)(2,1)} %get-tuple-element.61), calls=%async_computation.3 | async-start | bytes 8912896 | tf_op jit(solution)/shard_map/all_to_all | solution.py:149
  135.1 6.0 %fusion.1 = f32[4,16,4096]{2,1,0:T(8,128)} fusion(bf16[4,16,1024]{2,1,0:T(8,128)(2,1)S(1)} %dot_general.37, bf16[1024,4096]{1,0:T(8,128)(2,1)} %param.20), kind=kOutput, calls=%fused_computation.6 | convolution fusion | flops 536870912 | bytes 9568256 | tf_op jit(solution)/shard_map/dot_general | solution.py:132
  141.3 0.8 gather_fusion.2
  142.3 27.8 %reduce-scatter.2.cloned.1.call-done = f32[4,16,1024]{2,1,0:T(8,128)} async-done(((f32[4,16,4096]{2,1,0:T(8,128)}), f32[4,16,1024]{2,1,0:T(8,128)}) %reduce-scatter.2.cloned.1.call-update) | async-done | bytes 262160 | tf_op jit(solution)/shard_map/reduce_scatter | solution.py:135
  170.1 1.8 multiply_reduce_fusion
  171.9 9.2 %all-reduce.1 = (f32[4,16]{1,0:T(4,128)S(1)}, f32[4,16]{1,0:T(4,128)S(1)}) all-reduce(f32[4,16]{1,0:T(4,128)S(1)} %get-tuple-element.41, f32[4,16]{1,0:T(4,128)S(1)} %get-tuple-element.40), channel_id=1, replica_groups=mesh['dom'=8,'tp'=4] {'tp'}, use_global_device_ids=true, to_apply=%region_12.13 | all-reduce | flops 128 | bytes 1024 | tf_op jit(solution)/shard_map/psum | solution.py:138
  181.7 12.4 %pmax.7 = f32[]{:T(128)} all-reduce(f32[]{:T(128)} %get-tuple-element.52), channel_id=1, replica_groups=mesh['dom'=8,'tp'=4] {'dom'}, use_global_device_ids=true, to_apply=%region_17.18 | all-reduce | flops 1 | bytes 8 | tf_op jit(solution)/shard_map/pmax | solution.py:144
  194.2 1.2 exponential_reduce_fusion
  195.4 12.5 %psum.23 = f32[]{:T(128)} all-reduce(f32[]{:T(128)} %exponential_reduce_fusion), channel_id=1, replica_groups=mesh['dom'=8,'tp'=4] {'dom'}, use_global_device_ids=true, to_apply=%region_19.20 | all-reduce | flops 1 | bytes 8 | tf_op jit(solution)/shard_map/psum | solution.py:145
  209.8 7.6 %scatter_fusion = bf16[16,132,256]{2,1,0:T(8,128)(2,1)S(1)} fusion(bf16[16,132,256]{2,1,0:T(8,128)(2,1)S(1)} %broadcast.504.clone, s32[64]{0:T(128)S(1)} %fusion.29, bf16[64,132,256]{2,1,0:T(8,128)(2,1)} %all-to-all-done.1), kind=kCustom, calls=%fused_computation.3 | custom fusion | bytes 12976384 | tf_op jit(solution)/shard_map/scatter | solution.py:82
  217.4 1.2 copy.66
  218.7 7.6 %scatter_fusion.1 = bf16[16,132,256]{2,1,0:T(8,128)(2,1)S(1)} fusion(bf16[16,132,256]{2,1,0:T(8,128)(2,1)S(1)} %broadcast.504.clone.1, s32[64]{0:T(128)S(1)} %fusion.29, bf16[64,132,256]{2,1,0:T(8,128)(2,1)} %all-to-all-done.2), kind=kCustom, calls=%fused_computation.4 | custom fusion | bytes 12976384 | tf_op jit(solution)/shard_map/scatter | solution.py:82
  226.3 1.2 copy.67
  (76 shorter events, 6.1 us)
Async XLA Ops:
  7.2 51.0 %copy-start = (bf16[4096,256]{1,0:T(8,128)(2,1)S(1)}, bf16[4096,256]{1,0:T(8,128)(2,1)}, u32[]{:S(2)}) copy-start(bf16[4096,256]{1,0:T(8,128)(2,1)} %param.19) | copy-start | bytes 6291460
  22.9 50.3 %all-to-all-start = ((bf16[8,8,1]{1,2,0:T(2,128)(2,1)}), bf16[8,8,1]{1,2,0:T(2,128)(2,1)S(1)}, u32[]{:S(2)}, u32[]{:S(2)}) async-start(bf16[8,8,1]{1,2,0:T(2,128)(2,1)} %fusion.23), calls=%async_computation.1 | async-start | bytes 8192 | tf_op jit(solution)/shard_map/all_to_all | solution.py:150
  50.9 4.2 %copy-start.9 = (f32[4096]{0:T(1024)S(1)}, f32[4096]{0:T(1024)}, u32[]{:S(2)}) copy-start(f32[4096]{0:T(1024)} %param.16) | copy-start | bytes 49156
  55.3 2.9 %copy-start.3 = (bf16[4,16,4096]{2,1,0:T(8,128)(2,1)}, bf16[4,16,4096]{2,1,0:T(8,128)(2,1)S(1)}, u32[]{:S(2)}) copy-start(bf16[4,16,4096]{2,1,0:T(8,128)(2,1)S(1)} %fusion.12) | copy-start | bytes 1572868
  58.2 1.2 copy-start.6
  58.2 1.5 copy-start.7
  73.2 56.5 %all-to-all-start.1 = ((bf16[64,132,256]{2,1,0:T(8,128)(2,1)}), bf16[64,132,256]{2,1,0:T(8,128)(2,1)}, u32[]{:S(2)}, u32[]{:S(2)}) async-start(bf16[64,132,256]{2,1,0:T(8,128)(2,1)} %get-tuple-element.62), calls=%async_computation.2 | async-start | bytes 8912896 | tf_op jit(solution)/shard_map/all_to_all | solution.py:148
  79.4 11.3 %copy-start.4 = (bf16[4,16,4096]{2,1,0:T(8,128)(2,1)S(1)}, bf16[4,16,4096]{2,1,0:T(8,128)(2,1)}, u32[]{:S(2)}) copy-start(bf16[4,16,4096]{2,1,0:T(8,128)(2,1)} %copy-done.3) | copy-start | bytes 1572868
  90.7 6.5 %copy-start.5 = (bf16[16,132,2,128]{3,2,1,0:T(2,128)(2,1)S(1)}, bf16[16,132,2,128]{3,2,1,0:T(2,128)(2,1)}, u32[]{:S(2)}) copy-start(bf16[16,132,2,128]{3,2,1,0:T(2,128)(2,1)} %reshape.513) | copy-start | bytes 3244036
  129.8 4.7 %copy-start.13 = (f32[4,16,2,4,132]{4,3,0,2,1:T(4,128)S(1)}, f32[4,16,2,4,132]{4,3,0,2,1:T(4,128)}, u32[]{:S(2)}) copy-start(f32[4,16,2,4,132]{4,3,0,2,1:T(4,128)} %get-tuple-element.66) | copy-start | bytes 811012
  129.8 88.8 %all-to-all-start.2 = ((bf16[64,132,256]{2,1,0:T(8,128)(2,1)}), bf16[64,132,256]{2,1,0:T(8,128)(2,1)}, u32[]{:S(2)}, u32[]{:S(2)}) async-start(bf16[64,132,256]{2,1,0:T(8,128)(2,1)} %get-tuple-element.61), calls=%async_computation.3 | async-start | bytes 8912896 | tf_op jit(solution)/shard_map/all_to_all | solution.py:149
  134.5 35.6 %reduce-scatter.2.cloned.1.call-start = ((), (), s32[]{:S(2)}) async-start(), calls=%async_computation.4 | async-start | bytes 1310720 | tf_op jit(solution)/shard_map/reduce_scatter | solution.py:135
  135.1 6.0 %copy-start.11 = (s32[4,16]{1,0:T(4,128)S(1)}, s32[4,16]{1,0:T(4,128)}, u32[]{:S(2)}) copy-start(s32[4,16]{1,0:T(4,128)} %param.23) | copy-start | bytes 772
  135.1 6.1 %copy-start.2 = (bf16[128256]{0:T(1024)(128)(2,1)S(1)}, bf16[128256]{0:T(1024)(128)(2,1)}, u32[]{:S(2)}) copy-start(bf16[128256]{0:T(1024)(128)(2,1)} %param.24) | copy-start | bytes 769540
  141.1 29.0 %copy-start.8 = (bf16[4,16,1024]{2,1,0:T(8,128)(2,1)S(1)}, bf16[4,16,1024]{2,1,0:T(8,128)(2,1)}, u32[]{:S(2)}) copy-start(bf16[4,16,1024]{2,1,0:T(8,128)(2,1)} %param.15) | copy-start | bytes 393220
  141.1 29.0 %copy-start.10 = (f32[1024]{0:T(1024)S(1)}, f32[1024]{0:T(1024)}, u32[]{:S(2)}) copy-start(f32[1024]{0:T(1024)} %param.25) | copy-start | bytes 12292
  141.1 40.0 %copy-start.12 = (f32[16]{0:T(128)S(1)}, f32[16]{0:T(128)}, u32[]{:S(2)}) copy-start(f32[16]{0:T(128)} %param.26) | copy-start | bytes 196
  218.7 8.8 %copy-start.1 = (bf16[4096,256]{1,0:T(8,128)(2,1)S(1)}, bf16[4096,256]{1,0:T(8,128)(2,1)}, u32[]{:S(2)}) copy-start(bf16[4096,256]{1,0:T(8,128)(2,1)} %param.19) | copy-start | bytes 6291460
Sparse Core Ops, SparseCore 0:
  141.3 28.7 reduce-scatter.1
where the time goes:
time: 236 us; the launch traced here: 234 us
  blocking collectives  60.3 us (26%)
  waiting for transfers between devices  58.6 us (25%)
  local copies, waits for them, and re-layouts  46.2 us (20%)
  starting transfers between devices  19.8 us (8%)
  matrix products  17.4 us (7%)
  other arithmetic  16.4 us (7%)
  between operations  15.7 us (7%)
    all_to_all x1, waiting for transfers between devices, local(): lax.all_to_all(pack_rows(key_rows), 'dom', split_axis=0, concat_axis=0, t...  30.7 us
    reduce_scatter x1, waiting for transfers between devices, local(): lax.psum_scatter(partial_value, 'tp', scatter_dimension=2, tiled=True)  27.8 us
    all_gather x1, blocking collectives, local(): gathered = lax.all_gather(activations, 'tp', axis=2, tiled=True)  16.7 us
    scatter x2, local copies, waits for them, and re-layouts, place_rows(): return blank.at[slot_index].set(tensor, mode='drop')  15.2 us
    psum x1, blocking collectives, local(): lax.psum(jnp.sum(jnp.exp(particle_log_weight - largest)), 'dom')  12.5 us
    pmax x1, blocking collectives, local(): largest = lax.pmax(jnp.max(particle_log_weight), 'dom')  12.4 us
    dot_general x1, local copies, waits for them, and re-layouts, local(): jnp.dot(flat_rows, w_query, preferred_element_type=jnp.float32)  11.3 us
    all_to_all x1, starting transfers between devices, local(): lax.all_to_all(arrival, 'dom', split_axis=0, concat_axis=0, tiled=True)  10.4 us
  transfers between devices with their start and end apart: 4, of which 2 were waited for; matrix products, arithmetic and copies ran while one was open for 27% of the time, Pallas kernels for 0%

commit v1 on v0

--- a/solution.py
+++ b/solution.py
@@ -81,7 +81,13 @@
         blank = jnp.zeros((particle_count,) + tensor.shape[1:], tensor.dtype)
         return blank.at[slot_index].set(tensor, mode="drop")
 
-    gathered = lax.all_gather(activations, "tp", axis=2, tiled=True)
+    size = lax.axis_size("tp")
+    current, blocks = (activations, [activations])
+    for _ in range(size - 1):
+        current = lax.ppermute(current, "tp", [(i, (i + 1) % size) for i in range(size)])
+        blocks.insert(0, current)
+    merged = jnp.concatenate(blocks, axis=2)
+    gathered = jnp.roll(merged, (lax.axis_index("tp") + 1) * activations.shape[2], axis=2)
     inputs = gathered.astype(jnp.float32)
     normed = (
         inputs * lax.rsqrt(jnp.mean(inputs * inputs, -1, keepdims=True) + 1e-05) * norm_gain

time: 236 us -> 229 us (0.970)
  blocking collectives: 60.3 us -> 42.2 us
  waiting for transfers between devices: 58.6 us -> 66.9 us
  starting transfers between devices: 19.8 us -> 24.4 us
  matrix products: 17.4 us -> 14.8 us
    all_gather x1 -> x0, blocking collectives: 16.7 us -> none  [local(): gathered = lax.all_gather(activations, 'tp', axis=2, tiled=True)]
    ppermute x0 -> x3, waiting for transfers between devices: none -> 8.02 us  [local(): lax.ppermute(current, 'tp', [(i, (i + 1) % size) for i in range(size)])]
    ppermute x0 -> x3, starting transfers between devices: none -> 4.74 us  [local(): lax.ppermute(current, 'tp', [(i, (i + 1) % size) for i in range(size)])]
    unnamed x33 -> x38, local copies, waits for them, and re-layouts: 5.91 us -> 6.1 us
  transfers between devices with their start and end apart: 4 -> 7, of which waited for: 2 -> 4; matrix products, arithmetic and copies ran while one was open for 27% -> 30% of each run, Pallas kernels for 0% -> 0%
where the time goes in v1:
time: 229 us; the launch traced here: 227 us
  waiting for transfers between devices  66.9 us (29%)
  local copies, waits for them, and re-layouts  46.2 us (20%)
  blocking collectives  42.2 us (18%)
  starting transfers between devices  24.4 us (11%)
  other arithmetic  17.1 us (7%)
  between operations  15.8 us (7%)
  matrix products  14.8 us (6%)
    all_to_all x1, waiting for transfers between devices, local(): lax.all_to_all(pack_rows(key_rows), 'dom', split_axis=0, concat_axis=0, t...  31.5 us
    reduce_scatter x1, waiting for transfers between devices, local(): lax.psum_scatter(partial_value, 'tp', scatter_dimension=2, tiled=True)  27.4 us
    scatter x2, local copies, waits for them, and re-layouts, place_rows(): return blank.at[slot_index].set(tensor, mode='drop')  15.2 us
    psum x1, blocking collectives, local(): lax.psum(jnp.sum(jnp.exp(particle_log_weight - largest)), 'dom')  12.5 us
    pmax x1, blocking collectives, local(): largest = lax.pmax(jnp.max(particle_log_weight), 'dom')  12.4 us
    dot_general x1, local copies, waits for them, and re-layouts, local(): jnp.dot(flat_rows, w_query, preferred_element_type=jnp.float32)  11.3 us
    all_to_all x1, starting transfers between devices, local(): lax.all_to_all(arrival, 'dom', split_axis=0, concat_axis=0, tiled=True)  10.4 us
    psum x1, blocking collectives, local(): lax.psum((jnp.sum(summed * twist_vec, -1), jnp.sum(summed * summed, -1)),...  9.26 us
  transfers between devices with their start and end apart: 7, of which 4 were waited for; matrix products, arithmetic and copies ran while one was open for 30% of the time, Pallas kernels for 0%

profile of v1, /device:TPU:0, one launch (start us, length us, event | category | flops | bytes accessed | tf_op | source)
XLA Modules:
  0.0 227.4 jit_solution(3006747422098504946)
XLA Ops:
  7.2 3.1 %collective-permute-start = (bf16[4,16,1024]{2,1,0:T(8,128)(2,1)}, bf16[4,16,1024]{2,1,0:T(8,128)(2,1)S(1)}, u32[]{:S(2)}, u32[]{:S(2)}) collective-permute-start(bf16[4,16,1024]{2,1,0:T(8,128)(2,1)} %param.15), channel_id=1, source_target_pairs={{0,1},{1,2},{2,3},{3,0},{4,5},{5,6},{6,7},{7,4},{8,9},{9,10},{10,1... | collective-permute-start | bytes 393224 | tf_op jit(solution)/shard_map/ppermute | solution.py:87
  11.2 1.3 fusion.34
  12.5 1.2 dynamic-slice
  13.7 1.4 dynamic-update-slice
  15.1 8.0 %all-reduce = s32[8]{0:T(128)S(1)} all-reduce(s32[8]{0:T(128)S(1)} %dynamic-update-slice), channel_id=1, replica_groups=mesh['dom'=8,'tp'=4] {'dom'}, use_global_device_ids=true, to_apply=%add | all-reduce | flops 8 | bytes 64
  23.1 1.3 fusion.23
  24.4 10.4 %all-to-all-start = ((bf16[8,8,1]{1,2,0:T(2,128)(2,1)}), bf16[8,8,1]{1,2,0:T(2,128)(2,1)S(1)}, u32[]{:S(2)}, u32[]{:S(2)}) async-start(bf16[8,8,1]{1,2,0:T(2,128)(2,1)} %fusion.23), calls=%async_computation.1 | async-start | bytes 8192 | tf_op jit(solution)/shard_map/all_to_all | solution.py:156
  35.7 1.6 collective-permute-start.1
  37.4 6.1 %collective-permute-done.1 = bf16[4,16,1024]{2,1,0:T(8,128)(2,1)S(1)} collective-permute-done((bf16[4,16,1024]{2,1,0:T(8,128)(2,1)S(1)}, bf16[4,16,1024]{2,1,0:T(8,128)(2,1)S(1)}, u32[]{:S(2)}, u32[]{:S(2)}) %collective-permute-start.1) | collective-permute-done | bytes 131104 | tf_op jit(solution)/shard_map/ppermute | solution.py:87
  44.2 4.2 %copy.75 = bf16[256,4096]{1,0:T(8,128)(2,1)} copy(bf16[256,4096]{0,1:T(8,128)(2,1)} %bitcast.59) | data formatting | bytes 4194304 | tf_op jit(solution)/shard_map/dot_general | solution.py:101
  48.4 1.9 collective-permute-done.2
  53.6 2.9 %gather_fusion = bf16[64,132,256]{2,1,0:T(8,128)(2,1)} fusion(bf16[16,132,256]{2,1,0:T(8,128)(2,1)S(1)} %pad_maximum_fusion.1, s32[1024]{0:T(1024)S(1)} %get-tuple-element.68), kind=kCustom, calls=%fused_computation | custom fusion | bytes 8651008 | tf_op jit(solution)/shard_map/gather | solution.py:78
  56.5 2.9 %gather_fusion.1 = bf16[64,132,256]{2,1,0:T(8,128)(2,1)} fusion(bf16[16,132,256]{2,1,0:T(8,128)(2,1)S(1)} %pad_maximum_fusion, s32[1024]{0:T(1024)S(1)} %get-tuple-element.68), kind=kCustom, calls=%fused_computation.1 | custom fusion | bytes 8651008 | tf_op jit(solution)/shard_map/gather | solution.py:78
  59.3 7.7 %broadcast_select_fusion = (bf16[64,132,256]{2,1,0:T(8,128)(2,1)}, bf16[64,132,256]{2,1,0:T(8,128)(2,1)}) fusion(bf16[64,132,256]{2,1,0:T(8,128)(2,1)} %gather_fusion.1, pred[64]{0:T(512)(128)(4,1)S(1)} %broadcast_compare_fusion, bf16[64,132,256]{2,1,0:T(8,128)(2,1)} %gather_fusion), kind=kLoop, calls=%fused_computation.8 | loop fusion | flops 4325376 | bytes 17301568 | tf_op jit(solution)/shard_map/jit(_where)/select_n | solution.py:78
  67.0 4.6 %all-to-all-start.1 = ((bf16[64,132,256]{2,1,0:T(8,128)(2,1)}), bf16[64,132,256]{2,1,0:T(8,128)(2,1)}, u32[]{:S(2)}, u32[]{:S(2)}) async-start(bf16[64,132,256]{2,1,0:T(8,128)(2,1)} %get-tuple-element.62), calls=%async_computation.2 | async-start | bytes 8912896 | tf_op jit(solution)/shard_map/all_to_all | solution.py:154
  71.6 11.3 %copy.81 = bf16[1024,4096]{1,0:T(8,128)(2,1)} copy(bf16[1024,4096]{0,1:T(8,128)(2,1)} %bitcast.57) | data formatting | bytes 16777216 | tf_op jit(solution)/shard_map/dot_general | solution.py:97
  83.0 1.2 reshape.513
  84.5 6.1 %fusion.13 = f32[4,16,8,128]{3,1,2,0:T(8,128)S(1)} fusion(bf16[8,128,4096,1]{2,1,0,3:T(8,128)(2,1)} %bitcast.58, bf16[4,16,4096]{2,1,0:T(8,128)(2,1)S(1)} %copy-done.5), kind=kOutput, calls=%fused_computation.27 | convolution fusion | flops 536870912 | bytes 9175040 | tf_op jit(solution)/shard_map/dot_general | solution.py:97
  90.9 1.1 fusion.35
  92.0 31.5 %all-to-all-done.1 = bf16[64,132,256]{2,1,0:T(8,128)(2,1)} async-done(((bf16[64,132,256]{2,1,0:T(8,128)(2,1)}), bf16[64,132,256]{2,1,0:T(8,128)(2,1)}, u32[]{:S(2)}, u32[]{:S(2)}) %all-to-all-start.1) | async-done | bytes 4325408 | tf_op jit(solution)/shard_map/all_to_all | solution.py:154
  123.5 4.6 %all-to-all-start.2 = ((bf16[64,132,256]{2,1,0:T(8,128)(2,1)}), bf16[64,132,256]{2,1,0:T(8,128)(2,1)}, u32[]{:S(2)}, u32[]{:S(2)}) async-start(bf16[64,132,256]{2,1,0:T(8,128)(2,1)} %get-tuple-element.61), calls=%async_computation.3 | async-start | bytes 8912896 | tf_op jit(solution)/shard_map/all_to_all | solution.py:155
  128.8 6.0 %fusion.1 = f32[4,16,4096]{2,1,0:T(8,128)} fusion(bf16[4,16,1024]{2,1,0:T(8,128)(2,1)S(1)} %dot_general.37, bf16[1024,4096]{1,0:T(8,128)(2,1)} %param.20), kind=kOutput, calls=%fused_computation.6 | convolution fusion | flops 536870912 | bytes 9568256 | tf_op jit(solution)/shard_map/dot_general | solution.py:138
  135.8 27.4 %reduce-scatter.2.cloned.1.call-done = f32[4,16,1024]{2,1,0:T(8,128)} async-done(((f32[4,16,4096]{2,1,0:T(8,128)}), f32[4,16,1024]{2,1,0:T(8,128)}) %reduce-scatter.2.cloned.1.call-update) | async-done | bytes 262160 | tf_op jit(solution)/shard_map/reduce_scatter | solution.py:141
  163.1 1.7 multiply_reduce_fusion
  164.9 9.3 %all-reduce.1 = (f32[4,16]{1,0:T(4,128)S(1)}, f32[4,16]{1,0:T(4,128)S(1)}) all-reduce(f32[4,16]{1,0:T(4,128)S(1)} %get-tuple-element.41, f32[4,16]{1,0:T(4,128)S(1)} %get-tuple-element.40), channel_id=1, replica_groups=mesh['dom'=8,'tp'=4] {'tp'}, use_global_device_ids=true, to_apply=%region_12.13 | all-reduce | flops 128 | bytes 1024 | tf_op jit(solution)/shard_map/psum | solution.py:144
  174.8 12.4 %pmax.7 = f32[]{:T(128)} all-reduce(f32[]{:T(128)} %get-tuple-element.52), channel_id=1, replica_groups=mesh['dom'=8,'tp'=4] {'dom'}, use_global_device_ids=true, to_apply=%region_17.18 | all-reduce | flops 1 | bytes 8 | tf_op jit(solution)/shard_map/pmax | solution.py:150
  187.2 1.2 exponential_reduce_fusion
  188.4 12.5 %psum.23 = f32[]{:T(128)} all-reduce(f32[]{:T(128)} %exponential_reduce_fusion), channel_id=1, replica_groups=mesh['dom'=8,'tp'=4] {'dom'}, use_global_device_ids=true, to_apply=%region_19.20 | all-reduce | flops 1 | bytes 8 | tf_op jit(solution)/shard_map/psum | solution.py:151
  202.9 7.6 %scatter_fusion = bf16[16,132,256]{2,1,0:T(8,128)(2,1)S(1)} fusion(bf16[16,132,256]{2,1,0:T(8,128)(2,1)S(1)} %broadcast.505.clone, s32[64]{0:T(128)S(1)} %fusion.29, bf16[64,132,256]{2,1,0:T(8,128)(2,1)} %all-to-all-done.1), kind=kCustom, calls=%fused_computation.3 | custom fusion | bytes 12976384 | tf_op jit(solution)/shard_map/scatter | solution.py:82
  210.4 1.2 copy.66
  211.7 7.6 %scatter_fusion.1 = bf16[16,132,256]{2,1,0:T(8,128)(2,1)S(1)} fusion(bf16[16,132,256]{2,1,0:T(8,128)(2,1)S(1)} %broadcast.505.clone.1, s32[64]{0:T(128)S(1)} %fusion.29, bf16[64,132,256]{2,1,0:T(8,128)(2,1)} %all-to-all-done.2), kind=kCustom, calls=%fused_computation.4 | custom fusion | bytes 12976384 | tf_op jit(solution)/shard_map/scatter | solution.py:82
  219.3 1.2 copy.67
  (86 shorter events, 9.3 us)
Async XLA Ops:
  7.2 44.8 %copy-start = (bf16[4096,256]{1,0:T(8,128)(2,1)S(1)}, bf16[4096,256]{1,0:T(8,128)(2,1)}, u32[]{:S(2)}) copy-start(bf16[4096,256]{1,0:T(8,128)(2,1)} %param.19) | copy-start | bytes 6291460
  7.2 28.6 %collective-permute-start = (bf16[4,16,1024]{2,1,0:T(8,128)(2,1)}, bf16[4,16,1024]{2,1,0:T(8,128)(2,1)S(1)}, u32[]{:S(2)}, u32[]{:S(2)}) collective-permute-start(bf16[4,16,1024]{2,1,0:T(8,128)(2,1)} %param.15), channel_id=1, source_target_pairs={{0,1},{1,2},{2,3},{3,0},{4,5},{5,6},{6,7},{7,4},{8,9},{9,10},{10,1... | collective-permute-start | bytes 393224 | tf_op jit(solution)/shard_map/ppermute | solution.py:87
  24.4 42.6 %all-to-all-start = ((bf16[8,8,1]{1,2,0:T(2,128)(2,1)}), bf16[8,8,1]{1,2,0:T(2,128)(2,1)S(1)}, u32[]{:S(2)}, u32[]{:S(2)}) async-start(bf16[8,8,1]{1,2,0:T(2,128)(2,1)} %fusion.23), calls=%async_computation.1 | async-start | bytes 8192 | tf_op jit(solution)/shard_map/all_to_all | solution.py:156
  35.7 7.8 %collective-permute-start.1 = (bf16[4,16,1024]{2,1,0:T(8,128)(2,1)S(1)}, bf16[4,16,1024]{2,1,0:T(8,128)(2,1)S(1)}, u32[]{:S(2)}, u32[]{:S(2)}) collective-permute-start(bf16[4,16,1024]{2,1,0:T(8,128)(2,1)S(1)} %collective-permute-done), channel_id=1, source_target_pairs={{0,1},{1,2},{2,3},{3,0},{4,5},{5,6},{6,7},{7,4},{8,9},{9,10},{10,1... | collective-permute-start | bytes 393224 | tf_op jit(solution)/shard_map/ppermute | solution.py:87
  43.5 6.8 %collective-permute-start.2 = (bf16[4,16,1024]{2,1,0:T(8,128)(2,1)S(1)}, bf16[4,16,1024]{2,1,0:T(8,128)(2,1)S(1)}, u32[]{:S(2)}, u32[]{:S(2)}) collective-permute-start(bf16[4,16,1024]{2,1,0:T(8,128)(2,1)S(1)} %collective-permute-done.1), channel_id=1, source_target_pairs={{0,1},{1,2},{2,3},{3,0},{4,5},{5,6},{6,7},{7,4},{8,9},{9,10},{10,1... | collective-permute-start | bytes 393224 | tf_op jit(solution)/shard_map/ppermute | solution.py:87
  44.2 6.2 %copy-start.6 = (bf16[4,16,1024]{2,1,0:T(8,128)(2,1)S(1)}, bf16[4,16,1024]{2,1,0:T(8,128)(2,1)}, u32[]{:S(2)}) copy-start(bf16[4,16,1024]{2,1,0:T(8,128)(2,1)} %param.15) | copy-start | bytes 393220
  48.3 2.3 %copy-start.10 = (f32[4096]{0:T(1024)S(1)}, f32[4096]{0:T(1024)}, u32[]{:S(2)}) copy-start(f32[4096]{0:T(1024)} %param.16) | copy-start | bytes 49156
  48.4 2.5 %copy-start.3 = (bf16[256,4096]{1,0:T(8,128)(2,1)S(1)}, bf16[256,4096]{1,0:T(8,128)(2,1)}, u32[]{:S(2)}) copy-start(bf16[256,4096]{1,0:T(8,128)(2,1)} %copy.75) | copy-start | bytes 6291460
  50.9 1.1 copy-start.4
  52.0 1.2 copy-start.8
  52.0 1.5 copy-start.9
  67.0 56.5 %all-to-all-start.1 = ((bf16[64,132,256]{2,1,0:T(8,128)(2,1)}), bf16[64,132,256]{2,1,0:T(8,128)(2,1)}, u32[]{:S(2)}, u32[]{:S(2)}) async-start(bf16[64,132,256]{2,1,0:T(8,128)(2,1)} %get-tuple-element.62), calls=%async_computation.2 | async-start | bytes 8912896 | tf_op jit(solution)/shard_map/all_to_all | solution.py:154
  83.0 1.5 copy-start.5
  84.5 6.4 %copy-start.7 = (bf16[16,132,2,128]{3,2,1,0:T(2,128)(2,1)S(1)}, bf16[16,132,2,128]{3,2,1,0:T(2,128)(2,1)}, u32[]{:S(2)}) copy-start(bf16[16,132,2,128]{3,2,1,0:T(2,128)(2,1)} %reshape.513) | copy-start | bytes 3244036
  123.5 88.1 %all-to-all-start.2 = ((bf16[64,132,256]{2,1,0:T(8,128)(2,1)}), bf16[64,132,256]{2,1,0:T(8,128)(2,1)}, u32[]{:S(2)}, u32[]{:S(2)}) async-start(bf16[64,132,256]{2,1,0:T(8,128)(2,1)} %get-tuple-element.61), calls=%async_computation.3 | async-start | bytes 8912896 | tf_op jit(solution)/shard_map/all_to_all | solution.py:155
  128.1 35.0 %reduce-scatter.2.cloned.1.call-start = ((), (), s32[]{:S(2)}) async-start(), calls=%async_computation.4 | async-start | bytes 1310720 | tf_op jit(solution)/shard_map/reduce_scatter | solution.py:141
  128.7 6.0 %copy-start.2 = (bf16[128256]{0:T(1024)(128)(2,1)S(1)}, bf16[128256]{0:T(1024)(128)(2,1)}, u32[]{:S(2)}) copy-start(bf16[128256]{0:T(1024)(128)(2,1)} %param.24) | copy-start | bytes 769540
  134.7 28.4 %copy-start.11 = (f32[1024]{0:T(1024)S(1)}, f32[1024]{0:T(1024)}, u32[]{:S(2)}) copy-start(f32[1024]{0:T(1024)} %param.25) | copy-start | bytes 12292
  134.7 39.4 %copy-start.12 = (f32[16]{0:T(128)S(1)}, f32[16]{0:T(128)}, u32[]{:S(2)}) copy-start(f32[16]{0:T(128)} %param.26) | copy-start | bytes 196
  211.7 8.8 %copy-start.1 = (bf16[4096,256]{1,0:T(8,128)(2,1)S(1)}, bf16[4096,256]{1,0:T(8,128)(2,1)}, u32[]{:S(2)}) copy-start(bf16[4096,256]{1,0:T(8,128)(2,1)} %param.19) | copy-start | bytes 6291460
Sparse Core Ops, SparseCore 0:
  134.9 28.1 reduce-scatter.1
